TPU v7x, 128 devices: a whole 4x4x4 slice. The times are simulated.
128 devices in a mesh: rows: 32 (over x, y, core), cores: 4 (over z).
Axes of the slice: x: 4, y: 4, z: 4, core: 2. Of those that a mesh axis runs over, the one named last changes fastest.
Arguments:
- rhs: float32 [524288, 128], P(('rows', 'cores')), may hold values from -6 to 6
- guess: float32 [524288, 128], P(('rows', 'cores')), may hold values from -4 to 4
- degree: float32 [524288], P(('rows', 'cores')), may hold values from 2 to 6
- weights: bfloat16 [4096, 16, 128, 128], P(('rows', 'cores')), may hold values from -0.1875 to 0.1875
- columns: int32 [4096, 16], P(('rows', 'cores')), may hold values from 0 to 287, as said below
- block_counts: int32 [4096], P(('rows', 'cores')), may hold values from 8 to 16, as said below
- send_lists: int32 [128, 128, 2], P(('rows', 'cores')), may hold values from 0 to 31
- aggregates: int32 [524288], P(('rows', 'cores')), may hold values from 0 to 16383
- coarse_diag: float32 [16384], replicated, may hold values from 4 to 32
Outputs:
- smoothed: float32 [524288, 128], P(('rows', 'cores'))
Inputs may be any that keep to these rules, and one draw needn't show every extreme that they name: `block_counts`: every block row has 8 or 16 live slots, and the rows of one device have exactly 320 live slots in all. `columns`: on every device, each table index from 32 up is named by at least one live slot.
All inputs are finite; a program needn't handle non-finite values.
Results may differ from a plain program's by a relative error of at most 0.0022.
Values may be sent and summed in bfloat16 or wider, within the bound.
A program may use at most 128 MiB of HBM per device.

v0:
```python
import jax
import jax.numpy as jnp
from jax import lax
from jax.sharding import PartitionSpec as P

NC = 16384
damping = 0.7


def body(rhs, guess, degree, weights, columns, block_counts, send_lists, aggregates, coarse_diag):
    nblocks = weights.shape[0]
    slots = weights.shape[1]
    blocksize = weights.shape[2]
    width = rhs.shape[1]
    my_lists = send_lists[0]
    flat_live = jnp.arange(slots, dtype=jnp.int32)[None, :] < block_counts[:, None]
    live_weights = weights * flat_live.astype(jnp.bfloat16)[:, :, None, None]

    def apply(field):
        blocks = field.astype(jnp.bfloat16).reshape(nblocks, blocksize, width)
        outgoing = blocks[my_lists]
        incoming = lax.all_to_all(
            outgoing, ("rows", "cores"), split_axis=0, concat_axis=0, tiled=True
        )
        table = jnp.concatenate([blocks, incoming.reshape(-1, blocksize, width)], 0)
        offsum = jnp.einsum(
            "bsij,bsjr->bir", live_weights, table[columns], preferred_element_type=jnp.float32
        )
        return degree[:, None] * field - offsum.reshape(-1, width)

    first = guess + damping * (rhs - apply(guess)) / degree[:, None]
    residue = rhs - apply(first)
    local_coarse = jax.ops.segment_sum(residue, aggregates, num_segments=NC)
    total = lax.psum(local_coarse, ("rows", "cores"))
    correction = (total / coarse_diag[:, None]).astype(jnp.bfloat16)
    second = first + correction[aggregates].astype(jnp.float32)
    return second + damping * (rhs - apply(second)) / degree[:, None]


def solution(mesh):
    return jax.shard_map(
        body,
        mesh=mesh,
        in_specs=(
            P(("rows", "cores"), None),
            P(("rows", "cores"), None),
            P(("rows", "cores")),
            P(("rows", "cores"), None, None, None),
            P(("rows", "cores"), None),
            P(("rows", "cores")),
            P(("rows", "cores"), None, None),
            P(("rows", "cores")),
            P(),
        ),
        out_specs=P(("rows", "cores"), None),
        check_vma=False,
    )
```

profile of v0, /device:TPU:1, one launch (start us, length us, event | category | flops | bytes accessed | tf_op | source)
XLA Modules:
  0.0 701.2 jit_solution(10539362851413579965)
XLA Ops:
  6.5 0.7 compare_select_fusion.2
  7.2 0.1 copy.10
  7.3 0.1 reshape.90
  7.5 1.7 convert_element_type.23
  9.2 8.6 %gather_fusion = bf16[256,128,128]{2,1,0:T(8,128)(2,1)} fusion(bf16[32,128,128]{2,1,0:T(8,128)(2,1)S(1)} %bitcast.53, s32[1024]{0:T(1024)S(1)} %pad_clamp_fusion.1), kind=kCustom, calls=%fused_computation | custom fusion | bytes 16778240 | tf_op jit(solution)/shard_map/gather | solution.py:21
  17.8 0.0 copy-start.8
  17.8 0.0 copy-start.9
  17.8 12.0 %all-to-all-start = ((bf16[128,2,128,128]{3,2,1,0:T(8,128)(2,1)}), bf16[128,2,128,128]{3,2,1,0:T(8,128)(2,1)}, u32[]{:S(2)}, u32[]{:S(2)}) async-start(bf16[128,2,128,128]{3,2,1,0:T(8,128)(2,1)} %bitcast.59), calls=%async_computation | async-start | bytes 16777216 | tf_op jit(solution)/shard_map/all_to_all | solution.py:22
  29.8 0.2 all-reduce.2.cloned.1.call-start
  30.0 0.0 copy-done.8
  30.0 0.1 copy.11
  30.1 0.1 reshape.98
  30.2 0.0 copy-done.9
  30.2 0.1 fusion.22
  30.3 100.4 %all-to-all-done = bf16[128,2,128,128]{3,2,1,0:T(8,128)(2,1)} async-done(((bf16[128,2,128,128]{3,2,1,0:T(8,128)(2,1)}), bf16[128,2,128,128]{3,2,1,0:T(8,128)(2,1)}, u32[]{:S(2)}, u32[]{:S(2)}) %all-to-all-start) | async-done | bytes 8388640 | tf_op jit(solution)/shard_map/all_to_all | solution.py:22
  130.7 7.8 %pad_maximum_fusion = bf16[288,128,128]{2,1,0:T(8,128)(2,1)} fusion(bf16[256,128,128]{2,1,0:T(8,128)(2,1)} %bitcast.3, bf16[32,128,128]{2,1,0:T(8,128)(2,1)S(1)} %bitcast.54), kind=kLoop, calls=%fused_computation.14 | loop fusion | flops 4718592 | bytes 18874368 | tf_op jit(solution)/shard_map/concatenate | solution.py:25
  138.5 17.6 %gather_fusion.1 = bf16[512,128,128]{2,1,0:T(8,128)(2,1)} fusion(bf16[288,128,128]{2,1,0:T(8,128)(2,1)} %pad_maximum_fusion, s32[1024]{0:T(1024)S(1)} %pad_clamp_fusion), kind=kCustom, calls=%fused_computation.1 | custom fusion | bytes 33556480 | tf_op jit(solution)/shard_map/gather | solution.py:27
  156.1 0.0 copy-start
  156.1 0.0 copy-start.4
  156.1 13.1 %fusion.4 = f32[32,128,128,1]{2,1,3,0:T(8,128)S(1)} fusion(bf16[32,16,128,128]{3,2,1,0:T(8,128)(2,1)} %bitcast.65, bf16[32,16,128,128]{3,2,1,0:T(8,128)(2,1)} %param.12, bf16[32,16]{1,0:T(8,128)(2,1)S(1)} %fusion.22), kind=kOutput, calls=%fused_computation.12 | convolution fusion | flops 2155872256 | bytes 35652608 | tf_op jit(solution)/shard_map/bsij,bsjr->bir/dot_general | solution.py:26
  169.2 0.0 copy-done
  169.2 0.0 copy-done.4
  169.2 0.0 copy-done.5
  169.3 1.0 fusion.23
  170.3 8.6 %gather_fusion.2 = bf16[256,128,128]{2,1,0:T(8,128)(2,1)} fusion(bf16[32,128,128]{2,1,0:T(8,128)(2,1)S(1)} %bitcast.55, s32[1024]{0:T(1024)S(1)} %pad_clamp_fusion.1), kind=kCustom, calls=%fused_computation.2 | custom fusion | bytes 16778240 | tf_op jit(solution)/shard_map/gather | solution.py:21
  178.9 111.8 %all_to_all.15 = bf16[128,2,128,128]{3,2,1,0:T(8,128)(2,1)} all-to-all(bf16[128,2,128,128]{3,2,1,0:T(8,128)(2,1)} %bitcast.63), channel_id=1, replica_groups=mesh['rows'=32,'cores'=4] {'rows','cores'}, dimensions={0} | all-to-all | bytes 16777216 | tf_op jit(solution)/shard_map/all_to_all | solution.py:22
  290.8 7.8 %pad_maximum_fusion.1 = bf16[288,128,128]{2,1,0:T(8,128)(2,1)} fusion(bf16[256,128,128]{2,1,0:T(8,128)(2,1)} %bitcast.60, bf16[32,128,128]{2,1,0:T(8,128)(2,1)S(1)} %bitcast.56), kind=kLoop, calls=%fused_computation.15 | loop fusion | flops 4718592 | bytes 18874368 | tf_op jit(solution)/shard_map/concatenate | solution.py:25
  298.6 17.6 %gather_fusion.3 = bf16[512,128,128]{2,1,0:T(8,128)(2,1)} fusion(bf16[288,128,128]{2,1,0:T(8,128)(2,1)} %pad_maximum_fusion.1, s32[1024]{0:T(1024)S(1)} %pad_clamp_fusion), kind=kCustom, calls=%fused_computation.3 | custom fusion | bytes 33556480 | tf_op jit(solution)/shard_map/gather | solution.py:27
  316.2 13.1 %fusion.2 = f32[32,128,128,1]{2,1,3,0:T(8,128)S(1)} fusion(bf16[32,16,128,128]{3,2,1,0:T(8,128)(2,1)} %bitcast.66, bf16[32,16,128,128]{3,2,1,0:T(8,128)(2,1)} %param.12, bf16[32,16]{1,0:T(8,128)(2,1)S(1)} %fusion.22), kind=kOutput, calls=%fused_computation.10 | convolution fusion | flops 2155872256 | bytes 35652608 | tf_op jit(solution)/shard_map/bsij,bsjr->bir/dot_general | solution.py:26
  329.3 0.0 copy-start.7
  329.3 0.0 copy-done.1
  329.3 2.0 fusion.15
  331.3 0.0 copy-done.7
  331.3 26.4 %scatter_custom_fusion = f32[16384,128]{1,0:T(8,128)} fusion(s32[4096]{0:T(1024)S(1)} %copy-done.7, f32[4096,128]{1,0:T(8,128)} %fusion.15, f32[]{:T(128)} %constant.2.clone.1), kind=kCustom, calls=%fused_computation.21 | custom fusion | flops 524288 | bytes 8389120 | tf_op jit(solution)/shard_map/scatter-add | solution.py:33
  357.7 0.0 all-reduce.2.cloned.1.call-update
  357.8 156.8 %all-reduce.2.cloned.1.call-done = f32[16384,128]{1,0:T(8,128)} async-done(((f32[16384,128]{1,0:T(8,128)}), f32[16384,128]{1,0:T(8,128)}) %all-reduce.2.cloned.1.call-update) | async-done | bytes 8388624 | tf_op jit(solution)/shard_map/psum | solution.py:34
  514.6 0.0 copy-done.6
  514.6 6.9 divide_convert_fusion
  521.5 17.1 %gather_fusion.4 = bf16[4096,128]{1,0:T(8,128)(2,1)} fusion(bf16[16384,128]{1,0:T(8,128)(2,1)} %divide_convert_fusion, s32[4096]{0:T(1024)S(1)} %fusion.21), kind=kCustom, calls=%fused_computation.4 | custom fusion | bytes 2113536 | tf_op jit(solution)/shard_map/gather | solution.py:36
  538.6 1.4 fusion.20
  540.0 8.6 %gather_fusion.5 = bf16[256,128,128]{2,1,0:T(8,128)(2,1)} fusion(bf16[32,128,128]{2,1,0:T(8,128)(2,1)S(1)} %bitcast.57, s32[1024]{0:T(1024)S(1)} %pad_clamp_fusion.1), kind=kCustom, calls=%fused_computation.5 | custom fusion | bytes 16778240 | tf_op jit(solution)/shard_map/gather | solution.py:21
  548.6 105.2 %all_to_all.16 = bf16[128,2,128,128]{3,2,1,0:T(8,128)(2,1)} all-to-all(bf16[128,2,128,128]{3,2,1,0:T(8,128)(2,1)} %bitcast.62), channel_id=1, replica_groups=mesh['rows'=32,'cores'=4] {'rows','cores'}, dimensions={0} | all-to-all | bytes 16777216 | tf_op jit(solution)/shard_map/all_to_all | solution.py:22
  653.8 7.8 %pad_maximum_fusion.2 = bf16[288,128,128]{2,1,0:T(8,128)(2,1)} fusion(bf16[256,128,128]{2,1,0:T(8,128)(2,1)} %bitcast.61, bf16[32,128,128]{2,1,0:T(8,128)(2,1)S(1)} %bitcast.58), kind=kLoop, calls=%fused_computation.16 | loop fusion | flops 4718592 | bytes 18874368 | tf_op jit(solution)/shard_map/concatenate | solution.py:25
  661.6 17.6 %gather_fusion.6 = bf16[512,128,128]{2,1,0:T(8,128)(2,1)} fusion(bf16[288,128,128]{2,1,0:T(8,128)(2,1)} %pad_maximum_fusion.2, s32[1024]{0:T(1024)S(1)} %pad_clamp_fusion), kind=kCustom, calls=%fused_computation.6 | custom fusion | bytes 33556480 | tf_op jit(solution)/shard_map/gather | solution.py:27
  679.2 13.1 %fusion = f32[32,128,128,1]{2,1,3,0:T(8,128)S(1)} fusion(bf16[32,16,128,128]{3,2,1,0:T(8,128)(2,1)} %bitcast.64, bf16[32,16,128,128]{3,2,1,0:T(8,128)(2,1)} %param.12, bf16[32,16]{1,0:T(8,128)(2,1)S(1)} %fusion.22), kind=kOutput, calls=%fused_computation.8 | convolution fusion | flops 2155872256 | bytes 35652608 | tf_op jit(solution)/shard_map/bsij,bsjr->bir/dot_general | solution.py:26
  692.4 0.0 copy-done.2
  692.4 0.0 copy-done.3
  692.4 2.0 fusion.14
  (9 shorter events, 0.0 us)
Async XLA Ops:
  17.8 12.2 %copy-start.8 = (s32[32,16]{0,1:T(8,128)S(1)}, s32[32,16]{0,1:T(8,128)}, u32[]{:S(2)}) copy-start(s32[32,16]{0,1:T(8,128)} %param.13) | copy-start | bytes 6148
  17.8 12.4 %copy-start.9 = (s32[32]{0:T(128)S(1)}, s32[32]{0:T(128)}, u32[]{:S(2)}) copy-start(s32[32]{0:T(128)} %param.14) | copy-start | bytes 388
  17.8 112.9 %all-to-all-start = ((bf16[128,2,128,128]{3,2,1,0:T(8,128)(2,1)}), bf16[128,2,128,128]{3,2,1,0:T(8,128)(2,1)}, u32[]{:S(2)}, u32[]{:S(2)}) async-start(bf16[128,2,128,128]{3,2,1,0:T(8,128)(2,1)} %bitcast.59), calls=%async_computation | async-start | bytes 16777216 | tf_op jit(solution)/shard_map/all_to_all | solution.py:22
  29.8 484.8 %all-reduce.2.cloned.1.call-start = ((), (), s32[]{:S(2)}) async-start(), calls=%async_computation.3 | async-start | bytes 16777216 | tf_op jit(solution)/shard_map/psum | solution.py:34
  156.1 13.1 %copy-start = (f32[4096,128]{1,0:T(8,128)S(1)}, f32[4096,128]{1,0:T(8,128)}, u32[]{:S(2)}) copy-start(f32[4096,128]{1,0:T(8,128)} %param.9) | copy-start | bytes 6291460
  156.1 13.1 %copy-start.4 = (f32[4096,128]{1,0:T(8,128)S(1)}, f32[4096,128]{1,0:T(8,128)}, u32[]{:S(2)}) copy-start(f32[4096,128]{1,0:T(8,128)} %param.10) | copy-start | bytes 6291460
  156.1 13.1 %copy-start.5 = (f32[4096]{0:T(1024)S(1)}, f32[4096]{0:T(1024)}, u32[]{:S(2)}) copy-start(f32[4096]{0:T(1024)} %param.11) | copy-start | bytes 49156
  316.2 13.1 %copy-start.1 = (f32[4096,128]{1,0:T(8,128)S(1)}, f32[4096,128]{1,0:T(8,128)}, u32[]{:S(2)}) copy-start(f32[4096,128]{1,0:T(8,128)} %param.9) | copy-start | bytes 6291460
  329.3 2.0 copy-start.7
  331.3 183.3 %copy-start.6 = (f32[16384]{0:T(1024)S(1)}, f32[16384]{0:T(1024)}, u32[]{:S(2)}) copy-start(f32[16384]{0:T(1024)} %param.17) | copy-start | bytes 196612
  679.2 13.1 %copy-start.2 = (f32[4096,128]{1,0:T(8,128)S(1)}, f32[4096,128]{1,0:T(8,128)}, u32[]{:S(2)}) copy-start(f32[4096,128]{1,0:T(8,128)} %param.9) | copy-start | bytes 6291460
  679.2 13.1 %copy-start.3 = (bf16[4096,128]{1,0:T(8,128)(2,1)S(1)}, bf16[4096,128]{1,0:T(8,128)(2,1)}, u32[]{:S(2)}) copy-start(bf16[4096,128]{1,0:T(8,128)(2,1)} %gather_fusion.4) | copy-start | bytes 3145732
Sparse Core Ops, SparseCore 0:
  357.9 156.6 all-reduce.1
where the time goes:
time: 702 us; the launch traced here: 701 us
  waiting for transfers between devices  257 us (37%)
  blocking collectives  217 us (31%)
  local copies, waits for them, and re-layouts  96.2 us (14%)
  other arithmetic  65.7 us (9%)
  matrix products  39.3 us (6%)
  between operations  13.6 us (2%)
  starting transfers between devices  12.2 us (2%)
    all_to_all x2, blocking collectives, apply(): lax.all_to_all(outgoing, ('rows', 'cores'), split_axis=0, concat_axis=0,...  217 us
    psum x1, waiting for transfers between devices, body(): total = lax.psum(local_coarse, ('rows', 'cores'))  157 us
    all_to_all x1, waiting for transfers between devices, apply(): lax.all_to_all(outgoing, ('rows', 'cores'), split_axis=0, concat_axis=0,...  100 us
    gather x3, local copies, waits for them, and re-layouts, apply(): table[columns]  52.8 us
    dot_general x3, matrix products, apply(): jnp.einsum('bsij,bsjr->bir', live_weights, table[columns], preferred_elem...  39.3 us
    scatter-add x1, other arithmetic, body(): local_coarse = jax.ops.segment_sum(residue, aggregates, num_segments=NC)  26.4 us
    gather x3, local copies, waits for them, and re-layouts, apply(): outgoing = blocks[my_lists]  25.8 us
    concatenate x3, other arithmetic, apply(): table = jnp.concatenate([blocks, incoming.reshape(-1, blocksize, width)], 0)  23.5 us
  transfers between devices with their start and end apart: 2, of which 2 were waited for; matrix products, arithmetic and copies ran while one was open for 0% of the time, Pallas kernels for 0%

commit v1 on v0

--- a/solution.py
+++ b/solution.py
@@ -1,3 +1,4 @@
+import functools
 import jax
 import jax.numpy as jnp
 from jax import lax
@@ -5,6 +6,15 @@
 
 NC = 16384
 damping = 0.7
+
+
+def turn_digits(xs, dev_axis, ax_name):
+    s_next = lax.psum(xs, dev_axis)
+    block_last = lax.psum(s_next, ax_name)
+    return block_last
+
+
+refer_views = functools.partial(turn_digits, dev_axis="cores", ax_name="rows")
 
 
 def body(rhs, guess, degree, weights, columns, block_counts, send_lists, aggregates, coarse_diag):
@@ -31,7 +41,7 @@
     first = guess + damping * (rhs - apply(guess)) / degree[:, None]
     residue = rhs - apply(first)
     local_coarse = jax.ops.segment_sum(residue, aggregates, num_segments=NC)
-    total = lax.psum(local_coarse, ("rows", "cores"))
+    total = refer_views(local_coarse)
     correction = (total / coarse_diag[:, None]).astype(jnp.bfloat16)
     second = first + correction[aggregates].astype(jnp.float32)
     return second + damping * (rhs - apply(second)) / degree[:, None]

time: 702 us -> 825 us (1.18)
  waiting for transfers between devices: 257 us -> 379 us
    psum x1 -> x2, waiting for transfers between devices: 157 us -> 279 us  [the longest x1 156 us: turn_digits(): s_next = lax.psum(xs, dev_axis)]
  transfers between devices with their start and end apart: 2 -> 3, of which waited for: 2 -> 3; matrix products, arithmetic and copies ran while one was open for 0% -> 0% of each run, Pallas kernels for 0% -> 0%
where the time goes in v1:
time: 825 us; the launch traced here: 824 us
  waiting for transfers between devices  379 us (46%)
  blocking collectives  218 us (26%)
  local copies, waits for them, and re-layouts  96.2 us (12%)
  other arithmetic  65.6 us (8%)
  matrix products  39.3 us (5%)
  between operations  13.6 us (2%)
  starting transfers between devices  12.5 us (2%)
    all_to_all x2, blocking collectives, apply(): lax.all_to_all(outgoing, ('rows', 'cores'), split_axis=0, concat_axis=0,...  218 us
    psum x1, waiting for transfers between devices, turn_digits(): s_next = lax.psum(xs, dev_axis)  156 us
    psum x1, waiting for transfers between devices, turn_digits(): block_last = lax.psum(s_next, ax_name)  123 us
    all_to_all x1, waiting for transfers between devices, apply(): lax.all_to_all(outgoing, ('rows', 'cores'), split_axis=0, concat_axis=0,...  100 us
    gather x3, local copies, waits for them, and re-layouts, apply(): table[columns]  52.8 us
    dot_general x3, matrix products, apply(): jnp.einsum('bsij,bsjr->bir', live_weights, table[columns], preferred_elem...  39.3 us
    scatter-add x1, other arithmetic, body(): local_coarse = jax.ops.segment_sum(residue, aggregates, num_segments=NC)  26.4 us
    gather x3, local copies, waits for them, and re-layouts, apply(): outgoing = blocks[my_lists]  25.8 us
  transfers between devices with their start and end apart: 3, of which 3 were waited for; matrix products, arithmetic and copies ran while one was open for 0% of the time, Pallas kernels for 0%

profile of v1, /device:TPU:1, one launch (start us, length us, event | category | flops | bytes accessed | tf_op | source)
XLA Modules:
  0.0 824.3 jit_solution(2202250085979300078)
XLA Ops:
  6.5 0.7 compare_select_fusion.2
  7.2 0.1 copy.10
  7.3 0.1 reshape.90
  7.5 1.7 convert_element_type.23
  9.2 8.6 %gather_fusion = bf16[256,128,128]{2,1,0:T(8,128)(2,1)} fusion(bf16[32,128,128]{2,1,0:T(8,128)(2,1)S(1)} %bitcast.53, s32[1024]{0:T(1024)S(1)} %pad_clamp_fusion.1), kind=kCustom, calls=%fused_computation | custom fusion | bytes 16778240 | tf_op jit(solution)/shard_map/gather | solution.py:31
  17.8 0.0 copy-start.8
  17.8 12.0 %all-to-all-start = ((bf16[128,2,128,128]{3,2,1,0:T(8,128)(2,1)}), bf16[128,2,128,128]{3,2,1,0:T(8,128)(2,1)}, u32[]{:S(2)}, u32[]{:S(2)}) async-start(bf16[128,2,128,128]{3,2,1,0:T(8,128)(2,1)} %bitcast.59), calls=%async_computation | async-start | bytes 16777216 | tf_op jit(solution)/shard_map/all_to_all | solution.py:32
  29.8 0.2 all-reduce.3.cloned.1.call-start
  30.0 0.0 copy-done.8
  30.0 0.1 copy.11
  30.1 0.1 reshape.98
  30.2 0.0 copy-done.9
  30.2 0.1 fusion.22
  30.3 100.4 %all-to-all-done = bf16[128,2,128,128]{3,2,1,0:T(8,128)(2,1)} async-done(((bf16[128,2,128,128]{3,2,1,0:T(8,128)(2,1)}), bf16[128,2,128,128]{3,2,1,0:T(8,128)(2,1)}, u32[]{:S(2)}, u32[]{:S(2)}) %all-to-all-start) | async-done | bytes 8388640 | tf_op jit(solution)/shard_map/all_to_all | solution.py:32
  130.7 7.8 pad_maximum_fusion
  138.5 17.6 %gather_fusion.1 = bf16[512,128,128]{2,1,0:T(8,128)(2,1)} fusion(bf16[288,128,128]{2,1,0:T(8,128)(2,1)} %pad_maximum_fusion, s32[1024]{0:T(1024)S(1)} %pad_clamp_fusion), kind=kCustom, calls=%fused_computation.1 | custom fusion | bytes 33556480 | tf_op jit(solution)/shard_map/gather | solution.py:37
  156.1 13.1 %fusion.4 = f32[32,128,128,1]{2,1,3,0:T(8,128)S(1)} fusion(bf16[32,16,128,128]{3,2,1,0:T(8,128)(2,1)} %bitcast.65, bf16[32,16,128,128]{3,2,1,0:T(8,128)(2,1)} %param.12, bf16[32,16]{1,0:T(8,128)(2,1)S(1)} %fusion.22), kind=kOutput, calls=%fused_computation.12 | convolution fusion | flops 2155872256 | bytes 35652608 | tf_op jit(solution)/shard_map/bsij,bsjr->bir/dot_general | solution.py:36
  169.2 0.0 copy-done
  169.2 0.0 copy-done.4
  169.2 0.0 copy-done.5
  169.3 1.0 fusion.23
  170.3 8.6 %gather_fusion.2 = bf16[256,128,128]{2,1,0:T(8,128)(2,1)} fusion(bf16[32,128,128]{2,1,0:T(8,128)(2,1)S(1)} %bitcast.55, s32[1024]{0:T(1024)S(1)} %pad_clamp_fusion.1), kind=kCustom, calls=%fused_computation.2 | custom fusion | bytes 16778240 | tf_op jit(solution)/shard_map/gather | solution.py:31
  178.9 111.8 %all_to_all.15 = bf16[128,2,128,128]{3,2,1,0:T(8,128)(2,1)} all-to-all(bf16[128,2,128,128]{3,2,1,0:T(8,128)(2,1)} %bitcast.63), channel_id=1, replica_groups=mesh['rows'=32,'cores'=4] {'rows','cores'}, dimensions={0} | all-to-all | bytes 16777216 | tf_op jit(solution)/shard_map/all_to_all | solution.py:32
  290.8 7.8 pad_maximum_fusion.1
  298.6 17.6 %gather_fusion.3 = bf16[512,128,128]{2,1,0:T(8,128)(2,1)} fusion(bf16[288,128,128]{2,1,0:T(8,128)(2,1)} %pad_maximum_fusion.1, s32[1024]{0:T(1024)S(1)} %pad_clamp_fusion), kind=kCustom, calls=%fused_computation.3 | custom fusion | bytes 33556480 | tf_op jit(solution)/shard_map/gather | solution.py:37
  316.2 13.1 %fusion.2 = f32[32,128,128,1]{2,1,3,0:T(8,128)S(1)} fusion(bf16[32,16,128,128]{3,2,1,0:T(8,128)(2,1)} %bitcast.66, bf16[32,16,128,128]{3,2,1,0:T(8,128)(2,1)} %param.12, bf16[32,16]{1,0:T(8,128)(2,1)S(1)} %fusion.22), kind=kOutput, calls=%fused_computation.10 | convolution fusion | flops 2155872256 | bytes 35652608 | tf_op jit(solution)/shard_map/bsij,bsjr->bir/dot_general | solution.py:36
  329.3 0.0 copy-start.7
  329.3 0.0 copy-done.1
  329.3 2.0 fusion.15
  331.3 0.0 copy-done.7
  331.3 26.4 %scatter_custom_fusion = f32[16384,128]{1,0:T(8,128)} fusion(s32[4096]{0:T(1024)S(1)} %copy-done.7, f32[4096,128]{1,0:T(8,128)} %fusion.15, f32[]{:T(128)} %constant.2.clone.1), kind=kCustom, calls=%fused_computation.21 | custom fusion | flops 524288 | bytes 8389120 | tf_op jit(solution)/shard_map/scatter-add | solution.py:43
  357.7 0.0 all-reduce.3.cloned.1.call-update
  357.8 0.3 all-reduce.5.cloned.1.call-start
  358.1 155.5 %all-reduce.3.cloned.1.call-done = f32[16384,128]{1,0:T(8,128)} async-done(((f32[16384,128]{1,0:T(8,128)}), f32[16384,128]{1,0:T(8,128)}) %all-reduce.3.cloned.1.call-update) | async-done | bytes 8388624 | tf_op jit(solution)/shard_map/psum | solution.py:12
  513.6 0.0 all-reduce.5.cloned.1.call-update
  513.6 123.0 %all-reduce.5.cloned.1.call-done = f32[16384,128]{1,0:T(8,128)} async-done(((f32[16384,128]{1,0:T(8,128)}), f32[16384,128]{1,0:T(8,128)}) %all-reduce.5.cloned.1.call-update) | async-done | bytes 8388624 | tf_op jit(solution)/shard_map/psum | solution.py:13
  636.6 0.0 copy-done.6
  636.6 6.8 divide_convert_fusion
  643.5 17.1 %gather_fusion.4 = bf16[4096,128]{1,0:T(8,128)(2,1)} fusion(bf16[16384,128]{1,0:T(8,128)(2,1)} %divide_convert_fusion, s32[4096]{0:T(1024)S(1)} %fusion.21), kind=kCustom, calls=%fused_computation.4 | custom fusion | bytes 2113536 | tf_op jit(solution)/shard_map/gather | solution.py:46
  660.6 1.4 fusion.20
  662.0 8.6 %gather_fusion.5 = bf16[256,128,128]{2,1,0:T(8,128)(2,1)} fusion(bf16[32,128,128]{2,1,0:T(8,128)(2,1)S(1)} %bitcast.57, s32[1024]{0:T(1024)S(1)} %pad_clamp_fusion.1), kind=kCustom, calls=%fused_computation.5 | custom fusion | bytes 16778240 | tf_op jit(solution)/shard_map/gather | solution.py:31
  670.6 106.2 %all_to_all.16 = bf16[128,2,128,128]{3,2,1,0:T(8,128)(2,1)} all-to-all(bf16[128,2,128,128]{3,2,1,0:T(8,128)(2,1)} %bitcast.62), channel_id=1, replica_groups=mesh['rows'=32,'cores'=4] {'rows','cores'}, dimensions={0} | all-to-all | bytes 16777216 | tf_op jit(solution)/shard_map/all_to_all | solution.py:32
  776.9 7.8 pad_maximum_fusion.2
  784.7 17.6 %gather_fusion.6 = bf16[512,128,128]{2,1,0:T(8,128)(2,1)} fusion(bf16[288,128,128]{2,1,0:T(8,128)(2,1)} %pad_maximum_fusion.2, s32[1024]{0:T(1024)S(1)} %pad_clamp_fusion), kind=kCustom, calls=%fused_computation.6 | custom fusion | bytes 33556480 | tf_op jit(solution)/shard_map/gather | solution.py:37
  802.3 13.1 %fusion = f32[32,128,128,1]{2,1,3,0:T(8,128)S(1)} fusion(bf16[32,16,128,128]{3,2,1,0:T(8,128)(2,1)} %bitcast.64, bf16[32,16,128,128]{3,2,1,0:T(8,128)(2,1)} %param.12, bf16[32,16]{1,0:T(8,128)(2,1)S(1)} %fusion.22), kind=kOutput, calls=%fused_computation.8 | convolution fusion | flops 2155872256 | bytes 35652608 | tf_op jit(solution)/shard_map/bsij,bsjr->bir/dot_general | solution.py:36
  815.4 0.0 copy-done.2
  815.4 0.0 copy-done.3
  815.5 2.0 fusion.14
  (12 shorter events, 0.0 us)
Async XLA Ops:
  17.8 12.2 %copy-start.8 = (s32[32,16]{0,1:T(8,128)S(1)}, s32[32,16]{0,1:T(8,128)}, u32[]{:S(2)}) copy-start(s32[32,16]{0,1:T(8,128)} %param.13) | copy-start | bytes 6148
  17.8 12.4 %copy-start.9 = (s32[32]{0:T(128)S(1)}, s32[32]{0:T(128)}, u32[]{:S(2)}) copy-start(s32[32]{0:T(128)} %param.14) | copy-start | bytes 388
  17.8 112.9 %all-to-all-start = ((bf16[128,2,128,128]{3,2,1,0:T(8,128)(2,1)}), bf16[128,2,128,128]{3,2,1,0:T(8,128)(2,1)}, u32[]{:S(2)}, u32[]{:S(2)}) async-start(bf16[128,2,128,128]{3,2,1,0:T(8,128)(2,1)} %bitcast.59), calls=%async_computation | async-start | bytes 16777216 | tf_op jit(solution)/shard_map/all_to_all | solution.py:32
  29.8 483.8 %all-reduce.3.cloned.1.call-start = ((), (), s32[]{:S(2)}) async-start(), calls=%async_computation.3 | async-start | bytes 16777216 | tf_op jit(solution)/shard_map/psum | solution.py:12
  156.1 13.1 %copy-start = (f32[4096,128]{1,0:T(8,128)S(1)}, f32[4096,128]{1,0:T(8,128)}, u32[]{:S(2)}) copy-start(f32[4096,128]{1,0:T(8,128)} %param.9) | copy-start | bytes 6291460
  156.1 13.1 %copy-start.4 = (f32[4096,128]{1,0:T(8,128)S(1)}, f32[4096,128]{1,0:T(8,128)}, u32[]{:S(2)}) copy-start(f32[4096,128]{1,0:T(8,128)} %param.10) | copy-start | bytes 6291460
  156.1 13.1 %copy-start.5 = (f32[4096]{0:T(1024)S(1)}, f32[4096]{0:T(1024)}, u32[]{:S(2)}) copy-start(f32[4096]{0:T(1024)} %param.11) | copy-start | bytes 49156
  316.2 13.1 %copy-start.1 = (f32[4096,128]{1,0:T(8,128)S(1)}, f32[4096,128]{1,0:T(8,128)}, u32[]{:S(2)}) copy-start(f32[4096,128]{1,0:T(8,128)} %param.9) | copy-start | bytes 6291460
  329.3 2.0 copy-start.7
  357.7 278.9 %copy-start.6 = (f32[16384]{0:T(1024)S(1)}, f32[16384]{0:T(1024)}, u32[]{:S(2)}) copy-start(f32[16384]{0:T(1024)} %param.17) | copy-start | bytes 196612
  357.8 278.9 %all-reduce.5.cloned.1.call-start = ((), (), s32[]{:S(2)}) async-start(), calls=%async_computation.4 | async-start | bytes 16777216 | tf_op jit(solution)/shard_map/psum | solution.py:13
  802.3 13.1 %copy-start.2 = (f32[4096,128]{1,0:T(8,128)S(1)}, f32[4096,128]{1,0:T(8,128)}, u32[]{:S(2)}) copy-start(f32[4096,128]{1,0:T(8,128)} %param.9) | copy-start | bytes 6291460
  802.3 13.1 %copy-start.3 = (bf16[4096,128]{1,0:T(8,128)(2,1)S(1)}, bf16[4096,128]{1,0:T(8,128)(2,1)}, u32[]{:S(2)}) copy-start(bf16[4096,128]{1,0:T(8,128)(2,1)} %gather_fusion.4) | copy-start | bytes 3145732
Sparse Core Ops, SparseCore 0:
  357.9 155.6 all-reduce.2
  516.9 119.6 all-reduce.4
